TPU v7x, 32 devices: a whole 2x2x4 slice. The times are simulated.
32 devices in a mesh: leaf: 8 (over z, y), sub: 4 (over x, core).
Axes of the slice: x: 2, y: 2, z: 4, core: 2. Of those that a mesh axis runs over, the one named last changes fastest.
Arguments:
- signal: bfloat16 [32, 65536], P(None, ('leaf', 'sub')), may hold values from -6 to 6
- row_basis: bfloat16 [64, 65536], P(None, ('leaf', 'sub')), may hold values from -0.375 to 0.375
- transfer: bfloat16 [512, 9, 32, 128], P(('leaf', 'sub')), may hold values from -0.5 to 0.5
- column_basis: bfloat16 [64, 65536], P(None, ('leaf', 'sub')), may hold values from -0.75 to 0.75
- near_blocks: bfloat16 [768, 128, 256], P(('leaf', 'sub')), may hold values from -0.375 to 0.375
- near_list: int32 [768, 2], P(('leaf', 'sub')), may hold values from -1 to 31, as said below
Outputs:
- result: float32 [32, 65536], P(None, ('leaf', 'sub'))
Inputs may be any that keep to these rules, and one draw needn't show every extreme that they name: `near_list`: on each device the live entries (column >= 0) fill a leading run of its 24 slots, 2 or more of them, and empty slots hold -1 in both places; a live entry has 0 <= column < 24 and column <= row <= column + 8. Devices 2m and 2m + 1 hold at most 24 live entries together, and some such pair holds 24.
All inputs are finite; a program needn't handle non-finite values.
Results may differ from a plain program's by a relative error of at most 0.0003.
Values may be sent and summed in bfloat16 or wider, within the bound.
A program may use at most 128 MiB of HBM per device.

v0:
```python
import jax
import jax.numpy as jnp
from jax import lax
from jax.sharding import PartitionSpec as P

LEAF = 128


highest = lax.Precision.HIGHEST


def with_halo(cells, sides, width):
    for axis, dim in sides:
        count = lax.axis_size(axis)
        head = lax.slice_in_dim(cells, 0, width, axis=dim)
        tail = lax.slice_in_dim(cells, cells.shape[dim] - width, cells.shape[dim], axis=dim)
        cells = jnp.concatenate(
            [
                lax.ppermute(tail, axis, [(i, (i + 1) % count) for i in range(count)]),
                cells,
                lax.ppermute(head, axis, [((i + 1) % count, i) for i in range(count)]),
            ],
            axis=dim,
        )
    return cells


def swapped(shard, axis, distance):
    return lax.ppermute(shard, axis, [(i, i ^ 1 << distance) for i in range(lax.axis_size(axis))])


def from_behind(value, axis, steps):
    count = lax.axis_size(axis)
    pairs = [(source, (source + steps) % count) for source in range(count)]
    return lax.ppermute(value, axis, pairs)


def project(signal, row_basis):
    rhs_count = signal.shape[0] // 2
    rank_width = row_basis.shape[0] // 2
    leaves = signal.shape[1] // LEAF
    samples = signal.reshape(2, rhs_count, leaves, LEAF)
    basis_rows = row_basis.reshape(2, rank_width, leaves, LEAF)
    products = jnp.einsum(
        "xrlp,yqlp->xylrq", samples, basis_rows, preferred_element_type=jnp.float32
    )
    real_part = products[0, 0] + products[1, 1]
    imag_part = products[1, 0] - products[0, 1]
    return jnp.transpose(jnp.concatenate([real_part, imag_part], axis=-1), (1, 0, 2))


def block_form(weights):
    matrices = weights.astype(jnp.float32)
    rank_width = matrices.shape[1]
    pieces = []
    for offspring in range(2):
        real_part = matrices[:, :, 2 * offspring * rank_width : (2 * offspring + 1) * rank_width]
        imag_part = matrices[
            :, :, (2 * offspring + 1) * rank_width : (2 * offspring + 2) * rank_width
        ]
        upper_rows = jnp.concatenate([real_part, -imag_part], axis=2)
        lower_rows = jnp.concatenate([imag_part, real_part], axis=2)
        pieces.append(jnp.concatenate([upper_rows, lower_rows], axis=1))
    return jnp.concatenate(pieces, axis=1)


def apply_level(paired, weights):
    return jnp.einsum("rsm,smn->rsn", paired, block_form(weights), precision=highest)


def pair_local(coeffs, height):
    rhs_count, slot_count, doubled = coeffs.shape
    half_span = 2 ** (height - 1)
    grouped = coeffs.reshape(rhs_count, slot_count // (2 * half_span), 2, half_span, doubled)
    joined = jnp.concatenate([grouped[:, :, 0], grouped[:, :, 1]], axis=-1)
    twice = jnp.stack([joined, joined], axis=2)
    return twice.reshape(rhs_count, slot_count, 2 * doubled)


def swap_level(owned, partner_box, upper_bit, weights):
    low_side = jnp.where(upper_bit == 0, owned, partner_box)
    high_side = jnp.where(upper_bit == 0, partner_box, owned)
    return apply_level(jnp.concatenate([low_side, high_side], axis=-1), weights)


def evaluate(coeffs, column_basis):
    rhs_count, leaves, doubled = coeffs.shape
    rank_width = doubled // 2
    basis_rows = column_basis.astype(jnp.float32).reshape(2, rank_width, leaves, LEAF)
    real_coefficient = coeffs[:, :, :rank_width]
    imag_coef = coeffs[:, :, rank_width:]
    real_out = jnp.einsum(
        "rlq,qlp->rlp", real_coefficient, basis_rows[0], precision=highest
    ) - jnp.einsum("rlq,qlp->rlp", imag_coef, basis_rows[1], precision=highest)
    imag_out = jnp.einsum("rlq,qlp->rlp", imag_coef, basis_rows[0], precision=highest) + jnp.einsum(
        "rlq,qlp->rlp", real_coefficient, basis_rows[1], precision=highest
    )
    return jnp.concatenate([real_out, imag_out], axis=0).reshape(2 * rhs_count, leaves * LEAF)


def near_products(picked, blocks):
    products = jnp.einsum("scp,spj->scj", picked, blocks, preferred_element_type=jnp.float32)
    rhs_count = picked.shape[1] // 2
    real_part = products[:, :rhs_count, :LEAF] + products[:, rhs_count:, LEAF:]
    imag_part = products[:, rhs_count:, :LEAF] - products[:, :rhs_count, LEAF:]
    return jnp.concatenate([real_part, imag_part], axis=1)


def accumulate(output_values, col_index, box_count):
    selector = (col_index[:, None] == jnp.arange(box_count, dtype=jnp.int32)[None, :]).astype(
        jnp.float32
    )
    return jnp.einsum("sw,scj->cwj", selector, output_values, precision=highest)


def shards(signal, row_basis, transfer, column_basis, near_blocks, near_list):
    channels = signal.shape[0]
    box_count = signal.shape[1] // LEAF
    reach_boxes = box_count // 4
    local_levels = box_count.bit_length() - 1
    sub_bits = lax.axis_size("sub").bit_length() - 1
    count_of_leaves = lax.axis_size("leaf")
    leaf_bits = count_of_leaves.bit_length() - 1
    sub_index = lax.axis_index("sub")
    leaf_index = lax.axis_index("leaf")
    window = with_halo(signal, ((("leaf", "sub"), 1),), 2 * reach_boxes * LEAF)
    coeffs = project(signal, row_basis)
    for height in range(1, local_levels + 1):
        coeffs = apply_level(pair_local(coeffs, height), transfer[:, height - 1])
    for bit_place in range(sub_bits):
        partner_box = swapped(coeffs, "sub", bit_place)
        coeffs = swap_level(
            coeffs, partner_box, sub_index >> bit_place & 1, transfer[:, local_levels + bit_place]
        )
    for bit_place in range(leaf_bits):
        partner_box = swapped(coeffs, "leaf", bit_place)
        coeffs = swap_level(
            coeffs,
            partner_box,
            leaf_index >> bit_place & 1,
            transfer[:, local_levels + sub_bits + bit_place],
        )
    far_field = evaluate(coeffs, column_basis)
    leaf_tiles = window.reshape(channels, -1, LEAF)
    row_index = near_list[:, 0]
    col_index = near_list[:, 1]
    picked = jnp.transpose(jnp.take(leaf_tiles, jnp.maximum(row_index, 0), axis=1), (1, 0, 2))
    out_boxes = box_count + 2 * reach_boxes
    near_field = accumulate(near_products(picked, near_blocks), col_index, out_boxes)
    from_next = from_behind(near_field[:, :reach_boxes], ("leaf", "sub"), -1)
    from_prev = from_behind(near_field[:, box_count + reach_boxes :], ("leaf", "sub"), 1)
    center = near_field[:, reach_boxes : reach_boxes + box_count]
    center = center.at[:, :reach_boxes].add(from_prev)
    center = center.at[:, box_count - reach_boxes :].add(from_next)
    return far_field + center.reshape(channels, box_count * LEAF)


def solution(mesh):
    return jax.shard_map(
        shards,
        mesh=mesh,
        in_specs=(
            P(None, ("leaf", "sub")),
            P(None, ("leaf", "sub")),
            P(("leaf", "sub"), None, None, None),
            P(None, ("leaf", "sub")),
            P(("leaf", "sub"), None, None),
            P(("leaf", "sub"), None),
        ),
        out_specs=P(None, ("leaf", "sub")),
        check_vma=False,
    )
```

profile of v0, /device:TPU:0, one launch (start us, length us, event | category | flops | bytes accessed | tf_op | source)
XLA Modules:
  0.0 60.2 jit_solution(17310740215272328099)
XLA Ops:
  0.0 1.1 %copy.105 = bf16[8,8,16,128]{3,2,1,0:T(8,128)(2,1)S(1)} copy(bf16[8,8,16,128]{3,1,2,0:T(8,128)(2,1)} %bitcast.167) | data formatting | bytes 524288
  1.2 0.9 %copy.106 = bf16[4,8,16,128]{3,2,1,0:T(8,128)(2,1)S(1)} copy(bf16[4,8,16,128]{3,1,2,0:T(8,128)(2,1)} %bitcast.163) | data formatting | bytes 262144
  2.1 0.5 convolution_bitcast_fusion
  2.7 0.2 fusion.197
  2.9 0.3 copy.95
  3.3 0.2 slice_negate_fusion.1
  3.8 1.3 %fusion.124 = f32[16,64,16]{1,2,0:T(8,128)S(1)} fusion(f32[16,16,128]{2,0,1:T(8,128)S(1)} %bitcast.174, f32[16,32,32]{1,2,0:T(8,128)S(1)} %get-tuple-element.59, f32[16,32,32]{1,2,0:T(8,128)S(1)} %get-tuple-element.58, f32[16,32,32]{1,2,0:T(8,128)S(1)} %get-tuple-element.57, f32[16,32,32]{1,2,0:T(8,128)S(1)} %get-tuple-element.61, ...), kind=kOutput, calls=%fused_computation.134 | convolution fusion | flops 26083328 | bytes 589824 | tf_op jit(solution)/shard_map/rsm,smn->rsn/dot_general | solution.py:68
  5.2 0.3 copy.94
  5.7 1.3 %fusion.108 = f32[16,64,16]{1,2,0:T(8,128)S(1)} fusion(f32[16,16,128]{2,0,1:T(8,128)S(1)} %bitcast.169, f32[16,32,32]{1,2,0:T(8,128)S(1)} %get-tuple-element.53, f32[16,32,32]{1,2,0:T(8,128)S(1)} %get-tuple-element.52, f32[16,32,32]{1,2,0:T(8,128)S(1)} %get-tuple-element.51, f32[16,32,32]{1,2,0:T(8,128)S(1)} %get-tuple-element.55, ...), kind=kOutput, calls=%fused_computation.118 | convolution fusion | flops 26083328 | bytes 589824 | tf_op jit(solution)/shard_map/rsm,smn->rsn/dot_general | solution.py:68
  7.2 0.3 copy.93
  7.7 1.3 %fusion.92 = f32[16,64,16]{1,2,0:T(8,128)S(1)} fusion(f32[16,16,128]{2,0,1:T(8,128)S(1)} %bitcast.170, f32[16,32,32]{1,2,0:T(8,128)S(1)} %get-tuple-element.47, f32[16,32,32]{1,2,0:T(8,128)S(1)} %get-tuple-element.46, f32[16,32,32]{1,2,0:T(8,128)S(1)} %get-tuple-element.45, f32[16,32,32]{1,2,0:T(8,128)S(1)} %get-tuple-element.49, ...), kind=kOutput, calls=%fused_computation.102 | convolution fusion | flops 26083328 | bytes 589824 | tf_op jit(solution)/shard_map/rsm,smn->rsn/dot_general | solution.py:68
  9.1 0.3 copy.92
  9.7 1.3 %convolution_bitcast_fusion.6 = f32[16,16,64]{2,0,1:T(8,128)S(1)} fusion(f32[16,16,128]{2,0,1:T(8,128)S(1)} %bitcast.168, f32[16,32,32]{1,2,0:T(8,128)S(1)} %get-tuple-element.41, f32[16,32,32]{1,2,0:T(8,128)S(1)} %get-tuple-element.40, f32[16,32,32]{1,2,0:T(8,128)S(1)} %get-tuple-element.39, f32[16,32,32]{1,2,0:T(8,128)S(1)} %get-tuple-element.43, ...), kind=kOutput, calls=%fused_computation.7 | convolution fusion | flops 26083328 | bytes 589824 | tf_op jit(solution)/shard_map/rsm,smn->rsn/dot_general | solution.py:68
  11.0 0.5 collective-permute-start
  11.5 0.6 %fusion.199 = (bf16[32,1024]{1,0:T(8,128)(2,1)}, bf16[32,1024]{1,0:T(8,128)(2,1)S(1)}) fusion(bf16[32,2048]{1,0:T(8,128)(2,1)S(1)} %copy-done.2), kind=kLoop, calls=%fused_computation.284 | loop fusion | bytes 262144 | tf_op jit(solution)/shard_map/slice | solution.py:16
  12.2 6.6 %collective-permute-start.6 = (bf16[32,1024]{1,0:T(8,128)(2,1)S(1)}, bf16[32,1024]{1,0:T(8,128)(2,1)}, u32[]{:S(2)}, u32[]{:S(2)}) collective-permute-start(bf16[32,1024]{1,0:T(8,128)(2,1)S(1)} %get-tuple-element.117), channel_id=1, source_target_pairs={{1,0},{2,1},{3,2},{4,3},{5,4},{6,5},{7,6},{8,7},{9,8},{10,9},{11,1... | collective-permute-start | bytes 196616 | tf_op jit(solution)/shard_map/ppermute | solution.py:21
  18.7 0.3 copy.91
  19.1 1.2 %slice_negate_fusion.9 = (f32[16,32,32]{1,2,0:T(8,128)}, f32[16,32,32]{1,2,0:T(8,128)}, f32[16,32,32]{1,2,0:T(8,128)}, f32[16,32,32]{1,2,0:T(8,128)}, f32[16,32,32]{1,2,0:T(8,128)}, /*index=5*/f32[16,32,32]{1,2,0:T(8,128)}) fusion(f32[16,32,128]{1,2,0:T(8,128)S(1)} %bitcast_convert_fusion.4), kind=kLoop, calls=%fused_computation.273 | loop fusion | flops 32768 | bytes 655360 | tf_op jit(solution)/shard_map/neg | solution.py:61
  20.4 0.3 copy.90
  20.8 1.3 %slice_negate_fusion.11 = (f32[16,32,32]{1,2,0:T(8,128)}, f32[16,32,32]{1,2,0:T(8,128)}, f32[16,32,32]{1,2,0:T(8,128)}, f32[16,32,32]{1,2,0:T(8,128)}, f32[16,32,32]{1,2,0:T(8,128)}, /*index=5*/f32[16,32,32]{1,2,0:T(8,128)}) fusion(f32[16,32,128]{1,2,0:T(8,128)S(1)} %bitcast_convert_fusion.5), kind=kLoop, calls=%fused_computation.275 | loop fusion | flops 32768 | bytes 655360 | tf_op jit(solution)/shard_map/neg | solution.py:61
  22.0 0.3 copy.89
  22.4 1.2 %slice_negate_fusion.13 = (f32[16,32,32]{1,2,0:T(8,128)}, f32[16,32,32]{1,2,0:T(8,128)}, f32[16,32,32]{1,2,0:T(8,128)}, f32[16,32,32]{1,2,0:T(8,128)}, f32[16,32,32]{1,2,0:T(8,128)}, /*index=5*/f32[16,32,32]{1,2,0:T(8,128)}) fusion(f32[16,32,128]{1,2,0:T(8,128)S(1)} %bitcast_convert_fusion.6), kind=kLoop, calls=%fused_computation.277 | loop fusion | flops 32768 | bytes 655360 | tf_op jit(solution)/shard_map/neg | solution.py:61
  23.7 0.3 copy.88
  24.1 1.2 %slice_negate_fusion.15 = (f32[16,32,32]{1,2,0:T(8,128)}, f32[16,32,32]{1,2,0:T(8,128)}, f32[16,32,32]{1,2,0:T(8,128)}, f32[16,32,32]{1,2,0:T(8,128)}, f32[16,32,32]{1,2,0:T(8,128)}, /*index=5*/f32[16,32,32]{1,2,0:T(8,128)}) fusion(f32[16,32,128]{1,2,0:T(8,128)S(1)} %bitcast_convert_fusion.7), kind=kLoop, calls=%fused_computation.279 | loop fusion | flops 32768 | bytes 655360 | tf_op jit(solution)/shard_map/neg | solution.py:61
  25.3 0.3 copy.87
  25.8 1.0 %slice_negate_fusion.17 = (f32[16,32,32]{1,2,0:T(8,128)S(1)}, f32[16,32,32]{1,2,0:T(8,128)S(1)}, f32[16,32,32]{1,2,0:T(8,128)S(1)}, f32[16,32,32]{1,2,0:T(8,128)...) fusion(f32[16,32,128]{1,2,0:T(8,128)S(1)} %bitcast_convert_fusion.8), kind=kLoop, calls=%fused_computation.281 | loop fusion | flops 32768 | bytes 655360 | tf_op jit(solution)/shard_map/neg | solution.py:61
  26.8 0.9 %broadcast_select_fusion.1 = (f32[16,16,64]{2,0,1:T(8,128)S(1)}, f32[16,16,64]{2,0,1:T(8,128)S(1)}) fusion(f32[16,16,64]{2,0,1:T(8,128)S(1)} %convolution_bitcast_fusion.6, f32[16,16,64]{2,0,1:T(8,128)} %collective-permute-done, pred[]{:T(512)S(6)} %eq.39), kind=kLoop, calls=%fused_computation.237 | loop fusion | flops 32768 | bytes 262145 | tf_op jit(solution)/shard_map/jit(_where)/select_n | solution.py:81
  27.8 1.3 %convolution_bitcast_fusion.5 = f32[16,16,64]{2,0,1:T(8,128)S(1)} fusion(f32[16,32,32]{1,2,0:T(8,128)S(1)} %copy-done.26, f32[16,32,32]{1,2,0:T(8,128)S(1)} %copy-done.25, f32[16,32,32]{1,2,0:T(8,128)S(1)} %copy-done.24, f32[16,32,32]{1,2,0:T(8,128)S(1)} %copy-done.28, f32[16,32,32]{1,2,0:T(8,128)S(1)} %copy-done.27, f32[16,32,32]{1,2,0:T(8,128)S(1)} %copy-done.23, ...), kind=kOutput, calls=%fused_computation.6 | convolution fusion | flops 26116096 | bytes 589824 | tf_op jit(solution)/shard_map/rsm,smn->rsn/dot_general | solution.py:68
  29.2 0.9 %copy_bitcast_fusion.2 = bf16[32,32,128]{2,0,1:T(8,128)(2,1)S(1)} fusion(bf16[32,1024]{1,0:T(8,128)(2,1)} %collective-permute-done.6, bf16[32,2048]{1,0:T(8,128)(2,1)S(1)} %copy-done.2, bf16[32,1024]{1,0:T(8,128)(2,1)} %collective-permute-done.5), kind=kLoop, calls=%fused_computation.165 | loop fusion | flops 786432 | bytes 524288 | tf_op jit(solution)/shard_map/reshape | solution.py:144
  30.2 0.6 gather_fusion
  30.8 0.4 fusion.144
  31.3 0.5 fusion.140
  31.9 2.3 %collective-permute-done.1 = f32[16,16,64]{2,0,1:T(8,128)} collective-permute-done((f32[16,16,64]{2,0,1:T(8,128)S(1)}, f32[16,16,64]{2,0,1:T(8,128)}, u32[]{:S(2)}, u32[]{:S(2)}) %collective-permute-start.1) | collective-permute-done | bytes 65568 | tf_op jit(solution)/shard_map/ppermute | solution.py:29
  34.3 0.9 %broadcast_select_fusion.3 = (f32[16,16,64]{2,0,1:T(8,128)S(1)}, f32[16,16,64]{2,0,1:T(8,128)S(1)}) fusion(f32[16,16,64]{2,0,1:T(8,128)S(1)} %convolution_bitcast_fusion.5, f32[16,16,64]{2,0,1:T(8,128)} %collective-permute-done.1, pred[]{:T(512)S(6)} %eq.38), kind=kLoop, calls=%fused_computation.239 | loop fusion | flops 32768 | bytes 262145 | tf_op jit(solution)/shard_map/jit(_where)/select_n | solution.py:81
  35.3 1.3 %convolution_bitcast_fusion.4 = f32[16,16,64]{2,0,1:T(8,128)S(1)} fusion(f32[16,32,32]{1,2,0:T(8,128)S(1)} %copy-done.20, f32[16,32,32]{1,2,0:T(8,128)S(1)} %copy-done.19, f32[16,32,32]{1,2,0:T(8,128)S(1)} %copy-done.18, f32[16,32,32]{1,2,0:T(8,128)S(1)} %copy-done.22, f32[16,32,32]{1,2,0:T(8,128)S(1)} %copy-done.21, f32[16,32,32]{1,2,0:T(8,128)S(1)} %copy-done.17, ...), kind=kOutput, calls=%fused_computation.5 | convolution fusion | flops 26116096 | bytes 589824 | tf_op jit(solution)/shard_map/rsm,smn->rsn/dot_general | solution.py:68
  36.9 5.4 %collective-permute-start.8 = (f32[32,4,128]{2,0,1:T(8,128)S(1)}, f32[32,4,128]{2,0,1:T(8,128)S(1)}, u32[]{:S(2)}, u32[]{:S(2)}) collective-permute-start(f32[32,4,128]{2,0,1:T(8,128)S(1)} %get-tuple-element.94), channel_id=1, source_target_pairs={{0,31},{1,0},{2,1},{3,2},{4,3},{5,4},{6,5},{7,6},{8,7},{9,8},{10,9... | collective-permute-start | bytes 196616 | tf_op jit(solution)/shard_map/ppermute | solution.py:35
  42.3 1.3 %convolution_bitcast_fusion.3 = f32[16,16,64]{2,0,1:T(8,128)S(1)} fusion(f32[16,32,32]{1,2,0:T(8,128)S(1)} %copy-done.14, f32[16,32,32]{1,2,0:T(8,128)S(1)} %copy-done.13, f32[16,32,32]{1,2,0:T(8,128)S(1)} %copy-done.12, f32[16,32,32]{1,2,0:T(8,128)S(1)} %copy-done.16, f32[16,32,32]{1,2,0:T(8,128)S(1)} %copy-done.15, f32[16,32,32]{1,2,0:T(8,128)S(1)} %copy-done.11, ...), kind=kOutput, calls=%fused_computation.4 | convolution fusion | flops 26116096 | bytes 589824 | tf_op jit(solution)/shard_map/rsm,smn->rsn/dot_general | solution.py:68
  43.7 0.5 collective-permute-done.7
  44.2 4.4 %collective-permute-done.3 = f32[16,16,64]{2,0,1:T(8,128)S(1)} collective-permute-done((f32[16,16,64]{2,0,1:T(8,128)S(1)}, f32[16,16,64]{2,0,1:T(8,128)S(1)}, u32[]{:S(2)}, u32[]{:S(2)}) %collective-permute-start.3) | collective-permute-done | bytes 65568 | tf_op jit(solution)/shard_map/ppermute | solution.py:29
  48.7 1.3 %convolution_bitcast_fusion.2 = f32[16,16,64]{2,0,1:T(8,128)S(1)} fusion(f32[16,32,32]{1,2,0:T(8,128)S(1)} %copy-done.8, f32[16,32,32]{1,2,0:T(8,128)S(1)} %copy-done.7, f32[16,32,32]{1,2,0:T(8,128)S(1)} %copy-done.6, f32[16,32,32]{1,2,0:T(8,128)S(1)} %copy-done.10, f32[16,32,32]{1,2,0:T(8,128)S(1)} %copy-done.9, f32[16,32,32]{1,2,0:T(8,128)S(1)} %copy-done.5, ...), kind=kOutput, calls=%fused_computation.3 | convolution fusion | flops 26116096 | bytes 589824 | tf_op jit(solution)/shard_map/rsm,smn->rsn/dot_general | solution.py:68
  50.0 0.4 collective-permute-start.4
  50.4 6.6 %collective-permute-done.4 = f32[16,16,64]{2,0,1:T(8,128)S(1)} collective-permute-done((f32[16,16,64]{2,0,1:T(8,128)S(1)}, f32[16,16,64]{2,0,1:T(8,128)S(1)}, u32[]{:S(2)}, u32[]{:S(2)}) %collective-permute-start.4) | collective-permute-done | bytes 65568 | tf_op jit(solution)/shard_map/ppermute | solution.py:29
  57.1 1.3 %convolution_bitcast_fusion.1 = f32[16,16,64]{2,0,1:T(8,128)S(1)} fusion(f32[16,32,32]{1,2,0:T(8,128)S(1)} %get-tuple-element.89, f32[16,32,32]{1,2,0:T(8,128)S(1)} %get-tuple-element.88, f32[16,32,32]{1,2,0:T(8,128)S(1)} %get-tuple-element.87, f32[16,32,32]{1,2,0:T(8,128)S(1)} %copy-done.4, f32[16,32,32]{1,2,0:T(8,128)S(1)} %copy-done.3, ...), kind=kOutput, calls=%fused_computation.2 | convolution fusion | flops 26116096 | bytes 589824 | tf_op jit(solution)/shard_map/rsm,smn->rsn/dot_general | solution.py:68
  58.4 0.2 fusion.151
  58.6 0.3 fusion.149
  58.9 0.3 fusion.1
  59.2 0.2 fusion
  59.5 0.7 %copy_bitcast_fusion.1 = f32[32,2048]{1,0:T(8,128)} fusion(f32[32,16,128]{2,0,1:T(8,128)S(1)} %fusion.181, f32[16,16,128]{2,0,1:T(8,128)S(1)} %fusion, f32[16,16,128]{2,0,1:T(8,128)S(1)} %fusion.1), kind=kLoop, calls=%fused_computation.164 | loop fusion | flops 131072 | bytes 786432 | tf_op jit(solution)/shard_map/add | solution.py:155
  (118 shorter events, 2.7 us)
Async XLA Ops:
  0.0 30.7 %copy-start = (bf16[24,128,256]{2,1,0:T(8,128)(2,1)S(1)}, bf16[24,128,256]{2,1,0:T(8,128)(2,1)}, u32[]{:S(2)}) copy-start(bf16[24,128,256]{2,1,0:T(8,128)(2,1)} %param.14) | copy-start | bytes 4718596
  0.0 2.7 %copy-start.1 = (bf16[16,9,32,128]{3,2,1,0:T(8,128)(2,1)S(1)}, bf16[16,9,32,128]{3,2,1,0:T(8,128)(2,1)}, u32[]{:S(2)}) copy-start(bf16[16,9,32,128]{3,2,1,0:T(8,128)(2,1)} %param.12) | copy-start | bytes 3538948
  9.7 1.9 %copy-start.2 = (bf16[32,2048]{1,0:T(8,128)(2,1)S(1)}, bf16[32,2048]{1,0:T(8,128)(2,1)}, u32[]{:S(2)}) copy-start(bf16[32,2048]{1,0:T(8,128)(2,1)} %param.10) | copy-start | bytes 393220
  9.7 9.1 %copy-start.30 = (s32[24,2]{0,1:T(2,128)S(1)}, s32[24,2]{0,1:T(2,128)}, u32[]{:S(2)}) copy-start(s32[24,2]{0,1:T(2,128)} %param.15) | copy-start | bytes 580
  11.0 15.9 %collective-permute-start = (f32[16,16,64]{2,0,1:T(8,128)S(1)}, f32[16,16,64]{2,0,1:T(8,128)}, u32[]{:S(2)}, u32[]{:S(2)}) collective-permute-start(f32[16,16,64]{2,0,1:T(8,128)S(1)} %convolution_bitcast_fusion.6), channel_id=1, source_target_pairs={{0,1},{1,0},{2,3},{3,2},{4,5},{5,4},{6,7},{7,6},{8,9},{9,8},{10,11... | collective-permute-start | bytes 196616 | tf_op jit(solution)/shard_map/ppermute | solution.py:29
  12.1 17.1 %collective-permute-start.5 = (bf16[32,1024]{1,0:T(8,128)(2,1)}, bf16[32,1024]{1,0:T(8,128)(2,1)}, u32[]{:S(2)}, u32[]{:S(2)}) collective-permute-start(bf16[32,1024]{1,0:T(8,128)(2,1)} %get-tuple-element.116), channel_id=1, source_target_pairs={{0,1},{1,2},{2,3},{3,4},{4,5},{5,6},{6,7},{7,8},{8,9},{9,10},{10,1... | collective-permute-start | bytes 196616 | tf_op jit(solution)/shard_map/ppermute | solution.py:19
  12.2 17.1 %collective-permute-start.6 = (bf16[32,1024]{1,0:T(8,128)(2,1)S(1)}, bf16[32,1024]{1,0:T(8,128)(2,1)}, u32[]{:S(2)}, u32[]{:S(2)}) collective-permute-start(bf16[32,1024]{1,0:T(8,128)(2,1)S(1)} %get-tuple-element.117), channel_id=1, source_target_pairs={{1,0},{2,1},{3,2},{4,3},{5,4},{6,5},{7,6},{8,7},{9,8},{10,9},{11,1... | collective-permute-start | bytes 196616 | tf_op jit(solution)/shard_map/ppermute | solution.py:21
  25.7 1.1 %copy-start.29 = (bf16[64,2048]{1,0:T(8,128)(2,1)S(1)}, bf16[64,2048]{1,0:T(8,128)(2,1)}, u32[]{:S(2)}) copy-start(bf16[64,2048]{1,0:T(8,128)(2,1)} %param.13) | copy-start | bytes 786436
  25.7 2.1 %copy-start.23 = (f32[16,32,32]{1,2,0:T(8,128)S(1)}, f32[16,32,32]{1,2,0:T(8,128)}, u32[]{:S(2)}) copy-start(f32[16,32,32]{1,2,0:T(8,128)} %get-tuple-element.62) | copy-start | bytes 196612
  25.7 2.1 %copy-start.24 = (f32[16,32,32]{1,2,0:T(8,128)S(1)}, f32[16,32,32]{1,2,0:T(8,128)}, u32[]{:S(2)}) copy-start(f32[16,32,32]{1,2,0:T(8,128)} %get-tuple-element.63) | copy-start | bytes 196612
  25.7 2.1 %copy-start.25 = (f32[16,32,32]{1,2,0:T(8,128)S(1)}, f32[16,32,32]{1,2,0:T(8,128)}, u32[]{:S(2)}) copy-start(f32[16,32,32]{1,2,0:T(8,128)} %get-tuple-element.64) | copy-start | bytes 196612
  25.7 2.1 %copy-start.26 = (f32[16,32,32]{1,2,0:T(8,128)S(1)}, f32[16,32,32]{1,2,0:T(8,128)}, u32[]{:S(2)}) copy-start(f32[16,32,32]{1,2,0:T(8,128)} %get-tuple-element.65) | copy-start | bytes 196612
  25.8 2.1 %copy-start.27 = (f32[16,32,32]{1,2,0:T(8,128)S(1)}, f32[16,32,32]{1,2,0:T(8,128)}, u32[]{:S(2)}) copy-start(f32[16,32,32]{1,2,0:T(8,128)} %get-tuple-element.66) | copy-start | bytes 196612
  25.8 2.1 %copy-start.28 = (f32[16,32,32]{1,2,0:T(8,128)S(1)}, f32[16,32,32]{1,2,0:T(8,128)}, u32[]{:S(2)}) copy-start(f32[16,32,32]{1,2,0:T(8,128)} %get-tuple-element.67) | copy-start | bytes 196612
  29.1 5.1 %collective-permute-start.1 = (f32[16,16,64]{2,0,1:T(8,128)S(1)}, f32[16,16,64]{2,0,1:T(8,128)}, u32[]{:S(2)}, u32[]{:S(2)}) collective-permute-start(f32[16,16,64]{2,0,1:T(8,128)S(1)} %convolution_bitcast_fusion.5), channel_id=1, source_target_pairs={{0,2},{1,3},{2,0},{3,1},{4,6},{5,7},{6,4},{7,5},{8,10},{9,11},{10,... | collective-permute-start | bytes 196616 | tf_op jit(solution)/shard_map/ppermute | solution.py:29
  31.2 4.0 %copy-start.17 = (f32[16,32,32]{1,2,0:T(8,128)S(1)}, f32[16,32,32]{1,2,0:T(8,128)}, u32[]{:S(2)}) copy-start(f32[16,32,32]{1,2,0:T(8,128)} %get-tuple-element.68) | copy-start | bytes 196612
  31.2 4.0 %copy-start.18 = (f32[16,32,32]{1,2,0:T(8,128)S(1)}, f32[16,32,32]{1,2,0:T(8,128)}, u32[]{:S(2)}) copy-start(f32[16,32,32]{1,2,0:T(8,128)} %get-tuple-element.69) | copy-start | bytes 196612
  31.2 4.0 %copy-start.19 = (f32[16,32,32]{1,2,0:T(8,128)S(1)}, f32[16,32,32]{1,2,0:T(8,128)}, u32[]{:S(2)}) copy-start(f32[16,32,32]{1,2,0:T(8,128)} %get-tuple-element.70) | copy-start | bytes 196612
  31.2 4.0 %copy-start.20 = (f32[16,32,32]{1,2,0:T(8,128)S(1)}, f32[16,32,32]{1,2,0:T(8,128)}, u32[]{:S(2)}) copy-start(f32[16,32,32]{1,2,0:T(8,128)} %get-tuple-element.71) | copy-start | bytes 196612
  31.2 4.0 %copy-start.21 = (f32[16,32,32]{1,2,0:T(8,128)S(1)}, f32[16,32,32]{1,2,0:T(8,128)}, u32[]{:S(2)}) copy-start(f32[16,32,32]{1,2,0:T(8,128)} %get-tuple-element.72) | copy-start | bytes 196612
  31.3 4.0 %copy-start.22 = (f32[16,32,32]{1,2,0:T(8,128)S(1)}, f32[16,32,32]{1,2,0:T(8,128)}, u32[]{:S(2)}) copy-start(f32[16,32,32]{1,2,0:T(8,128)} %get-tuple-element.73) | copy-start | bytes 196612
  35.3 7.0 %copy-start.11 = (f32[16,32,32]{1,2,0:T(8,128)S(1)}, f32[16,32,32]{1,2,0:T(8,128)}, u32[]{:S(2)}) copy-start(f32[16,32,32]{1,2,0:T(8,128)} %get-tuple-element.74) | copy-start | bytes 196612
  35.3 7.0 %copy-start.12 = (f32[16,32,32]{1,2,0:T(8,128)S(1)}, f32[16,32,32]{1,2,0:T(8,128)}, u32[]{:S(2)}) copy-start(f32[16,32,32]{1,2,0:T(8,128)} %get-tuple-element.75) | copy-start | bytes 196612
  35.3 7.0 %copy-start.13 = (f32[16,32,32]{1,2,0:T(8,128)S(1)}, f32[16,32,32]{1,2,0:T(8,128)}, u32[]{:S(2)}) copy-start(f32[16,32,32]{1,2,0:T(8,128)} %get-tuple-element.76) | copy-start | bytes 196612
  35.3 7.0 %copy-start.14 = (f32[16,32,32]{1,2,0:T(8,128)S(1)}, f32[16,32,32]{1,2,0:T(8,128)}, u32[]{:S(2)}) copy-start(f32[16,32,32]{1,2,0:T(8,128)} %get-tuple-element.77) | copy-start | bytes 196612
  35.3 7.0 %copy-start.15 = (f32[16,32,32]{1,2,0:T(8,128)S(1)}, f32[16,32,32]{1,2,0:T(8,128)}, u32[]{:S(2)}) copy-start(f32[16,32,32]{1,2,0:T(8,128)} %get-tuple-element.78) | copy-start | bytes 196612
  35.3 7.0 %copy-start.16 = (f32[16,32,32]{1,2,0:T(8,128)S(1)}, f32[16,32,32]{1,2,0:T(8,128)}, u32[]{:S(2)}) copy-start(f32[16,32,32]{1,2,0:T(8,128)} %get-tuple-element.79) | copy-start | bytes 196612
  36.6 5.6 %collective-permute-start.2 = (f32[16,16,64]{2,0,1:T(8,128)S(1)}, f32[16,16,64]{2,0,1:T(8,128)S(1)}, u32[]{:S(2)}, u32[]{:S(2)}) collective-permute-start(f32[16,16,64]{2,0,1:T(8,128)S(1)} %convolution_bitcast_fusion.4), channel_id=1, source_target_pairs={{0,4},{4,0},{8,12},{12,8},{16,20},{20,16},{24,28},{28,24},{1,5},{5... | collective-permute-start | bytes 196616 | tf_op jit(solution)/shard_map/ppermute | solution.py:29
  36.7 7.4 %collective-permute-start.7 = (f32[32,4,128]{2,0,1:T(8,128)S(1)}, f32[32,4,128]{2,0,1:T(8,128)S(1)}, u32[]{:S(2)}, u32[]{:S(2)}) collective-permute-start(f32[32,4,128]{2,0,1:T(8,128)S(1)} %get-tuple-element.95), channel_id=1, source_target_pairs={{0,1},{1,2},{2,3},{3,4},{4,5},{5,6},{6,7},{7,8},{8,9},{9,10},{10,1... | collective-permute-start | bytes 196616 | tf_op jit(solution)/shard_map/ppermute | solution.py:35
  36.8 11.9 %copy-start.5 = (f32[16,32,32]{1,2,0:T(8,128)S(1)}, f32[16,32,32]{1,2,0:T(8,128)}, u32[]{:S(2)}) copy-start(f32[16,32,32]{1,2,0:T(8,128)} %get-tuple-element.80) | copy-start | bytes 196612
  36.8 11.9 %copy-start.6 = (f32[16,32,32]{1,2,0:T(8,128)S(1)}, f32[16,32,32]{1,2,0:T(8,128)}, u32[]{:S(2)}) copy-start(f32[16,32,32]{1,2,0:T(8,128)} %get-tuple-element.81) | copy-start | bytes 196612
  36.8 11.9 %copy-start.7 = (f32[16,32,32]{1,2,0:T(8,128)S(1)}, f32[16,32,32]{1,2,0:T(8,128)}, u32[]{:S(2)}) copy-start(f32[16,32,32]{1,2,0:T(8,128)} %get-tuple-element.82) | copy-start | bytes 196612
  36.8 11.9 %copy-start.8 = (f32[16,32,32]{1,2,0:T(8,128)S(1)}, f32[16,32,32]{1,2,0:T(8,128)}, u32[]{:S(2)}) copy-start(f32[16,32,32]{1,2,0:T(8,128)} %get-tuple-element.83) | copy-start | bytes 196612
  36.8 11.9 %copy-start.9 = (f32[16,32,32]{1,2,0:T(8,128)S(1)}, f32[16,32,32]{1,2,0:T(8,128)}, u32[]{:S(2)}) copy-start(f32[16,32,32]{1,2,0:T(8,128)} %get-tuple-element.84) | copy-start | bytes 196612
  36.9 11.9 %copy-start.10 = (f32[16,32,32]{1,2,0:T(8,128)S(1)}, f32[16,32,32]{1,2,0:T(8,128)}, u32[]{:S(2)}) copy-start(f32[16,32,32]{1,2,0:T(8,128)} %get-tuple-element.85) | copy-start | bytes 196612
  36.9 13.5 %collective-permute-start.8 = (f32[32,4,128]{2,0,1:T(8,128)S(1)}, f32[32,4,128]{2,0,1:T(8,128)S(1)}, u32[]{:S(2)}, u32[]{:S(2)}) collective-permute-start(f32[32,4,128]{2,0,1:T(8,128)S(1)} %get-tuple-element.94), channel_id=1, source_target_pairs={{0,31},{1,0},{2,1},{3,2},{4,3},{5,4},{6,5},{7,6},{8,7},{9,8},{10,9... | collective-permute-start | bytes 196616 | tf_op jit(solution)/shard_map/ppermute | solution.py:35
  43.6 5.0 %collective-permute-start.3 = (f32[16,16,64]{2,0,1:T(8,128)S(1)}, f32[16,16,64]{2,0,1:T(8,128)S(1)}, u32[]{:S(2)}, u32[]{:S(2)}) collective-permute-start(f32[16,16,64]{2,0,1:T(8,128)S(1)} %convolution_bitcast_fusion.3), channel_id=1, source_target_pairs={{0,8},{4,12},{8,0},{12,4},{16,24},{20,28},{24,16},{28,20},{1,9},{5... | collective-permute-start | bytes 196616 | tf_op jit(solution)/shard_map/ppermute | solution.py:29
  44.2 12.9 %copy-start.3 = (f32[16,32,32]{1,2,0:T(8,128)S(1)}, f32[16,32,32]{1,2,0:T(8,128)}, u32[]{:S(2)}) copy-start(f32[16,32,32]{1,2,0:T(8,128)} %get-tuple-element.90) | copy-start | bytes 196612
  44.2 12.9 %copy-start.4 = (f32[16,32,32]{1,2,0:T(8,128)S(1)}, f32[16,32,32]{1,2,0:T(8,128)}, u32[]{:S(2)}) copy-start(f32[16,32,32]{1,2,0:T(8,128)} %get-tuple-element.91) | copy-start | bytes 196612
  50.0 7.0 %collective-permute-start.4 = (f32[16,16,64]{2,0,1:T(8,128)S(1)}, f32[16,16,64]{2,0,1:T(8,128)S(1)}, u32[]{:S(2)}, u32[]{:S(2)}) collective-permute-start(f32[16,16,64]{2,0,1:T(8,128)S(1)} %convolution_bitcast_fusion.2), channel_id=1, source_target_pairs={{0,16},{4,20},{8,24},{12,28},{16,0},{20,4},{24,8},{28,12},{1,17},{... | collective-permute-start | bytes 196616 | tf_op jit(solution)/shard_map/ppermute | solution.py:29
where the time goes:
time: 60.4 us; the launch traced here: 60.2 us
  matrix products  14.1 us (23%)
  waiting for transfers between devices  13.9 us (23%)
  starting transfers between devices  13.1 us (22%)
  other arithmetic  11.7 us (19%)
  local copies, waits for them, and re-layouts  6.45 us (11%)
  between operations  0.98 us (2%)
    ppermute x5, waiting for transfers between devices, swapped(): lax.ppermute(shard, axis, [(i, i ^ 1 << distance) for i in range(lax.axis...  13.4 us
    dot_general x9, matrix products, apply_level(): jnp.einsum('rsm,smn->rsn', paired, block_form(weights), precision=highest)  11.6 us
    ppermute x1, starting transfers between devices, with_halo(): lax.ppermute(head, axis, [((i + 1) % count, i) for i in range(count)])  6.56 us
    neg x9, other arithmetic, block_form(): upper_rows = jnp.concatenate([real_part, -imag_part], axis=2)  6.54 us
    ppermute x2, starting transfers between devices, from_behind(): return lax.ppermute(value, axis, pairs)  5.41 us
    unnamed x74, local copies, waits for them, and re-layouts  4.77 us
    select_n x5, other arithmetic, swap_level(): low_side = jnp.where(upper_bit == 0, owned, partner_box)  1.92 us
  transfers between devices with their start and end apart: 9, of which 4 were waited for; matrix products, arithmetic and copies ran while one was open for 27% of the time, Pallas kernels for 0%

commit v1 on v0

v1 whole, which is shorter than its diff:
```python
import functools

import jax
import jax.numpy as jnp
from jax import lax
from jax.experimental import pallas as pl
from jax.experimental.pallas import tpu as pltpu
from jax.sharding import PartitionSpec as P

LEAF = 128
MESH = pl.DeviceIdType.MESH
F32 = jnp.float32
BF16 = jnp.bfloat16
CHUNKS = 2


def dot(a, b):
    return lax.dot_general(a, b, (((1,), (0,)), ((), ())), preferred_element_type=F32)


def dot_t(a, b):
    return lax.dot_general(a, b, (((1,), (1,)), ((), ())), preferred_element_type=F32)


def halves(value):
    high = value.astype(BF16)
    low = (value - high.astype(F32)).astype(BF16)
    return high, low


def product(value, matrix):
    rows = value.shape[0]
    both = dot(jnp.concatenate(halves(value), axis=0), matrix)
    return both[:rows] + both[rows:]


def kernel(
    leaf_count, sub_count,
    list_ref, signal_hbm, row_hbm, transfer_hbm, column_hbm, block_hbm, out_ref,
    win, row_basis, transfer, column_basis, blocks, spread, evals, sent, got, own, vals, near, edges,
    in_sems, send_sems, recv_sems, halo_send, halo_recv,
):
    boxes = signal_hbm.shape[1] // LEAF
    channels = signal_hbm.shape[0]
    rhs = channels // 2
    rank = row_hbm.shape[0] // 2
    wide = 2 * rank
    reach = boxes // 4
    pairs = boxes // 2
    local_levels = boxes.bit_length() - 1
    slots = block_hbm.shape[0]
    levels = transfer_hbm.shape[1]
    leaf = lax.axis_index("leaf")
    sub = lax.axis_index("sub")
    count = leaf_count * sub_count
    me = leaf * sub_count + sub
    after = lax.rem(me + 1, count)
    before = lax.rem(me + count - 1, count)
    next_id = (lax.div(after, sub_count), lax.rem(after, sub_count))
    prev_id = (lax.div(before, sub_count), lax.rem(before, sub_count))

    crossing = []
    for place in range(sub_count.bit_length() - 1):
        bit = lax.rem(lax.div(sub, 1 << place), 2)
        crossing.append((bit, (leaf, sub + (1 - 2 * bit) * (1 << place))))
    for place in range(leaf_count.bit_length() - 1):
        bit = lax.rem(lax.div(leaf, 1 << place), 2)
        crossing.append((bit, (leaf + (1 - 2 * bit) * (1 << place), sub)))
    partners = [partner for _, partner in crossing] + [next_id, prev_id]

    signal_copies = [
        pltpu.make_async_copy(
            signal_hbm.at[:, pl.ds(b * LEAF, LEAF)], win.at[2 * reach + b], in_sems.at[b]
        )
        for b in range(boxes)
    ]
    row_copy = pltpu.make_async_copy(row_hbm, row_basis, in_sems.at[boxes])
    column_copy = pltpu.make_async_copy(column_hbm, column_basis, in_sems.at[boxes + 1])
    block_copy = pltpu.make_async_copy(block_hbm, blocks, in_sems.at[boxes + 2])
    transfer_copies = [
        pltpu.make_async_copy(transfer_hbm.at[:, l], transfer.at[l], in_sems.at[boxes + 3 + l])
        for l in range(levels)
    ]
    for copy in signal_copies:
        copy.start()
    row_copy.start()
    for l in range(local_levels):
        transfer_copies[l].start()

    barrier = pltpu.get_barrier_semaphore()
    for partner in partners:
        pl.semaphore_signal(barrier, inc=1, device_id=partner, device_id_type=MESH)
    for l in range(local_levels, levels):
        transfer_copies[l].start()
    block_copy.start()
    column_copy.start()

    source = lax.broadcasted_iota(jnp.int32, (LEAF, 4 * LEAF), 0)
    target = lax.broadcasted_iota(jnp.int32, (LEAF, 4 * LEAF), 1)
    group = target // LEAF
    child = group // 2
    lower = group % 2
    lane = target % LEAF
    inner = lane % wide
    imag = inner // rank
    moved = inner + lower * (rank - 2 * rank * imag)
    sign = (1 - 2 * imag * (1 - lower)).astype(F32)
    hit = source == child * wide + moved
    moves = [
        jnp.where(hit & (lane // wide == half), sign, 0.0).astype(BF16) for half in range(2)
    ]

    def build(l):
        transfer_copies[l].wait()
        forms = []
        for half in range(2):
            weights = transfer[l, half * pairs : (half + 1) * pairs].reshape(pairs * rank, LEAF)
            forms.append(dot(weights, moves[half]))
        if l == local_levels - 1:
            full = (forms[0] + forms[1]).astype(BF16).reshape(pairs, rank, 4 * LEAF)
            for g in range(4):
                spread[l, 0, :, g * rank : (g + 1) * rank, :] = full[
                    :, :, g * LEAF : (g + 1) * LEAF
                ]
            return
        for half in range(2):
            form = forms[half].astype(BF16).reshape(pairs, rank, 4 * LEAF)
            for c in range(2):
                for part in range(2):
                    top = half * wide + part * rank
                    g = 2 * c + part
                    spread[l, c, :, top : top + rank, :] = form[:, :, g * LEAF : (g + 1) * LEAF]

    left = lax.broadcasted_iota(jnp.int32, (rhs, LEAF), 1) < wide

    for copy in signal_copies:
        copy.wait()
    pl.semaphore_wait(barrier, len(partners))
    halo = [
        pltpu.make_async_remote_copy(
            src_ref=win.at[pl.ds(boxes, 2 * reach)], dst_ref=win.at[pl.ds(0, 2 * reach)],
            send_sem=halo_send.at[0], recv_sem=halo_recv.at[0],
            device_id=next_id, device_id_type=MESH,
        ),
        pltpu.make_async_remote_copy(
            src_ref=win.at[pl.ds(2 * reach, 2 * reach)],
            dst_ref=win.at[pl.ds(2 * reach + boxes, 2 * reach)],
            send_sem=halo_send.at[1], recv_sem=halo_recv.at[1],
            device_id=prev_id, device_id_type=MESH,
        ),
    ]
    for copy in halo:
        copy.start()

    row_copy.wait()
    coeffs = []
    for k in range(pairs):
        real_side, imag_side = [], []
        for b in (k, k + pairs):
            basis = row_basis[:, b * LEAF : (b + 1) * LEAF]
            real_side += [basis[:rank], -basis[rank:]]
            imag_side += [basis[rank:], basis[:rank]]
        points = [win[2 * reach + b] for b in (k, k + pairs)]
        both = dot_t(
            jnp.concatenate([points[0][:rhs], points[1][:rhs]], axis=0),
            jnp.concatenate(real_side, axis=0),
        ) + dot_t(
            jnp.concatenate([points[0][rhs:], points[1][rhs:]], axis=0),
            jnp.concatenate(imag_side, axis=0),
        )
        coeffs.append(jnp.where(left, both[:rhs], both[rhs:]))

    for l in range(local_levels):
        build(l)
    for l in range(local_levels - 1):
        bit = 1 << l
        coeffs = [
            product(coeffs[k & ~bit], spread[l, 0, k]) + product(coeffs[k | bit], spread[l, 1, k])
            for k in range(pairs)
        ]
    last = local_levels - 1
    coeffs = [product(coeffs[k], spread[last, 0, k]) for k in range(pairs)]

    chunk = pairs // CHUNKS

    def exchange(i, part):
        span = pl.ds(part * chunk, chunk)
        return pltpu.make_async_remote_copy(
            src_ref=sent.at[i, span], dst_ref=got.at[i, span],
            send_sem=send_sems.at[i, part], recv_sem=recv_sems.at[i, part],
            device_id=crossing[i][1], device_id_type=MESH,
        )

    def near_products():
        for copy in halo:
            copy.wait_recv()
        block_copy.wait()
        for s in range(slots):
            picked = win[jnp.maximum(list_ref[s, 0], 0)]
            both = dot(picked, blocks[s])
            vals[s, :rhs] = both[:rhs, :LEAF] + both[rhs:, LEAF:]
            vals[s, rhs:] = both[rhs:, :LEAF] - both[:rhs, LEAF:]

    def near_sum(j):
        total = jnp.zeros((channels, LEAF), F32)
        for s in range(slots):
            total = total + jnp.where(list_ref[s, 1] == j, vals[s], 0.0)
        near[j] = total

    def near_sums(first, stop):
        def body(j, carry):
            near_sum(j)
            return carry

        lax.fori_loop(first, stop, body, 0)

    rim = [
        pltpu.make_async_remote_copy(
            src_ref=near.at[pl.ds(0, reach)], dst_ref=edges.at[1],
            send_sem=halo_send.at[2], recv_sem=halo_recv.at[2],
            device_id=prev_id, device_id_type=MESH,
        ),
        pltpu.make_async_remote_copy(
            src_ref=near.at[pl.ds(boxes + reach, reach)], dst_ref=edges.at[0],
            send_sem=halo_send.at[3], recv_sem=halo_recv.at[3],
            device_id=next_id, device_id_type=MESH,
        ),
    ]

    def near_edges():
        near_products()
        near_sums(0, reach)
        rim[0].start()
        near_sums(boxes + reach, boxes + 2 * reach)
        rim[1].start()

    def near_middle():
        near_sums(reach, boxes + reach)

    def build_evals():
        column_copy.wait()
        for k in range(pairs):
            for half in range(2):
                b = k + half * pairs
                basis = column_basis[:, b * LEAF : (b + 1) * LEAF]
                top = half * wide
                evals[k, top : top + rank, :LEAF] = basis[:rank]
                evals[k, top : top + rank, LEAF:] = basis[rank:]
                evals[k, top + rank : top + wide, :LEAF] = -basis[rank:]
                evals[k, top + rank : top + wide, LEAF:] = basis[:rank]

    steps = len(crossing)
    extra = [[] for _ in range(steps)]
    extra[min(1, steps - 1)].append(near_edges)
    extra[min(2, steps - 1)].append(near_middle)
    extra[min(3, steps - 1)].append(build_evals)

    for part in range(CHUNKS):
        for k in range(part * chunk, (part + 1) * chunk):
            sent[0, k] = coeffs[k]
        exchange(0, part).start()
    for i in range(steps):
        l = local_levels + i
        bit = crossing[i][0]
        build(l)
        for k in range(pairs):
            own[k] = product(sent[i, k], spread[l, bit, k])
        for work in extra[i]:
            work()
        if i == steps - 1:
            for copy in rim:
                copy.wait_recv()
        for part in range(CHUNKS):
            exchange(i, part).wait_recv()
            for k in range(part * chunk, (part + 1) * chunk):
                value = own[k] + product(got[i, k], spread[l, 1 - bit, k])
                if i < steps - 1:
                    sent[i + 1, k] = value
                    continue
                high, low = halves(value)
                zero = jnp.zeros_like(high)
                far = dot(
                    jnp.concatenate(
                        [
                            jnp.where(left, high, zero), jnp.where(left, low, zero),
                            jnp.where(left, zero, high), jnp.where(left, zero, low),
                        ],
                        axis=0,
                    ),
                    evals[k],
                )
                for half in range(2):
                    b = k + half * pairs
                    both = far[2 * half * rhs : (2 * half + 1) * rhs] + far[
                        (2 * half + 1) * rhs : (2 * half + 2) * rhs
                    ]
                    result = near[reach + b]
                    if b < reach:
                        result = result + edges[0, b]
                    if b >= boxes - reach:
                        result = result + edges[1, b - boxes + reach]
                    here = slice(b * LEAF, (b + 1) * LEAF)
                    out_ref[:rhs, here] = both[:, :LEAF] + result[:rhs]
                    out_ref[rhs:, here] = both[:, LEAF:] + result[rhs:]
            if i < steps - 1:
                exchange(i + 1, part).start()
    for i in range(steps):
        for part in range(CHUNKS):
            exchange(i, part).wait_send()
    for copy in halo + rim:
        copy.wait_send()


def solution(mesh):
    leaf_count, sub_count = mesh.shape["leaf"], mesh.shape["sub"]
    steps = leaf_count.bit_length() + sub_count.bit_length() - 2

    def shards(signal, row_basis, transfer, column_basis, near_blocks, near_list):
        channels, points = signal.shape
        boxes = points // LEAF
        reach, pairs = boxes // 4, boxes // 2
        rhs = channels // 2
        levels, rank = transfer.shape[1], transfer.shape[2]
        slots = near_blocks.shape[0]
        anywhere = pl.BlockSpec(memory_space=pl.ANY)
        return pl.pallas_call(
            functools.partial(kernel, leaf_count, sub_count),
            out_shape=jax.ShapeDtypeStruct((channels, points), F32),
            in_specs=[pl.BlockSpec(memory_space=pltpu.SMEM)] + [anywhere] * 5,
            out_specs=pl.BlockSpec(memory_space=pltpu.VMEM),
            scratch_shapes=[
                pltpu.VMEM((boxes + 4 * reach, channels, LEAF), BF16),
                pltpu.VMEM(row_basis.shape, BF16),
                pltpu.VMEM((levels, boxes, rank, LEAF), BF16),
                pltpu.VMEM(column_basis.shape, BF16),
                pltpu.VMEM(near_blocks.shape, BF16),
                pltpu.VMEM((levels, 2, pairs, LEAF, LEAF), BF16),
                pltpu.VMEM((pairs, LEAF, 2 * LEAF), BF16),
                pltpu.VMEM((steps, pairs, rhs, LEAF), F32),
                pltpu.VMEM((steps, pairs, rhs, LEAF), F32),
                pltpu.VMEM((pairs, rhs, LEAF), F32),
                pltpu.VMEM((slots, channels, LEAF), F32),
                pltpu.VMEM((boxes + 2 * reach, channels, LEAF), F32),
                pltpu.VMEM((2, reach, channels, LEAF), F32),
                pltpu.SemaphoreType.DMA((boxes + 3 + levels,)),
                pltpu.SemaphoreType.DMA((steps, CHUNKS)),
                pltpu.SemaphoreType.DMA((steps, CHUNKS)),
                pltpu.SemaphoreType.DMA((4,)),
                pltpu.SemaphoreType.DMA((4,)),
            ],
            compiler_params=pltpu.CompilerParams(
                collective_id=0, has_side_effects=True, vmem_limit_bytes=40 * 1024 * 1024
            ),
        )(near_list, signal, row_basis, transfer, column_basis, near_blocks)

    return jax.shard_map(
        shards,
        mesh=mesh,
        in_specs=(
            P(None, ("leaf", "sub")),
            P(None, ("leaf", "sub")),
            P(("leaf", "sub"), None, None, None),
            P(None, ("leaf", "sub")),
            P(("leaf", "sub"), None, None),
            P(("leaf", "sub"), None),
        ),
        out_specs=P(None, ("leaf", "sub")),
        check_vma=False,
    )
```

time: 60.4 us -> 30.2 us (0.50)
  Pallas kernels: 0 us -> 23 us
  matrix products: 14.1 us -> 0 us
  waiting for transfers between devices: 13.9 us -> 0 us
  starting transfers between devices: 13.1 us -> 0 us
  other arithmetic: 11.7 us -> 0 us
  between operations: 0.98 us -> 0.01 us
    pallas_call x0 -> x1, Pallas kernels: none -> 23 us  [shards(): pl.pallas_call(functools.partial(kernel, leaf_count, sub_count), out_shap...]
    dot_general x16 -> x0, matrix products: 14.1 us -> none  [the longest x9 11.6 us: apply_level(): jnp.einsum('rsm,smn->rsn', paired, block_form(weights), precision=highest)]
    ppermute x9 -> x0, waiting for transfers between devices: 13.9 us -> none  [the longest x5 13.4 us: swapped(): lax.ppermute(shard, axis, [(i, i ^ 1 << distance) for i in range(lax.axis...]
    ppermute x9 -> x0, starting transfers between devices: 13.1 us -> none  [the longest x1 6.56 us: with_halo(): lax.ppermute(head, axis, [((i + 1) % count, i) for i in range(count)])]
    neg x9 -> x0, other arithmetic: 6.54 us -> none  [block_form(): upper_rows = jnp.concatenate([real_part, -imag_part], axis=2)]
    unnamed x74 -> x12, local copies, waits for them, and re-layouts: 4.77 us -> 6.94 us
    select_n x5 -> x0, other arithmetic: 1.92 us -> none  [swap_level(): low_side = jnp.where(upper_bit == 0, owned, partner_box)]
    convert_element_type x9 -> x0, other arithmetic: 0.93 us -> none  [block_form(): matrices = weights.astype(jnp.float32)]
  transfers between devices with their start and end apart: 9 -> 0, of which waited for: 4 -> 0; matrix products, arithmetic and copies ran while one was open for 27% -> 0% of each run, Pallas kernels for 0% -> 0%
where the time goes in v1:
time: 30.2 us; the launch traced here: 29.9 us
  Pallas kernels  23 us (76%)
  local copies, waits for them, and re-layouts  6.94 us (23%)
    pallas_call x1, Pallas kernels, shards(): pl.pallas_call(functools.partial(kernel, leaf_count, sub_count), out_shap...  23 us
    unnamed x12, local copies, waits for them, and re-layouts  6.94 us

profile of v1, /device:TPU:0, one launch (start us, length us, event | category | flops | bytes accessed | tf_op | source)
XLA Modules:
  0.0 29.9 jit_solution(7240377763272920278)
XLA Ops:
  0.0 0.8 %copy.7.list_ref = s32[24,2]{1,0:T(8,128)S(1)} copy(s32[24,2]{0,1:T(2,128)} %param.11) | data formatting | bytes 384 | tf_op args[5]
  0.8 0.0 copy-start
  0.8 1.4 %copy-done = bf16[24,128,256]{2,1,0:T(8,128)(2,1)S(1)} copy-done((bf16[24,128,256]{2,1,0:T(8,128)(2,1)S(1)}, bf16[24,128,256]{2,1,0:T(8,128)(2,1)}, u32[]{:S(2)}) %copy-start) | copy-done | bytes 1572888
  2.2 0.0 copy-start.1
  2.2 1.3 %copy-done.1 = bf16[16,9,32,128]{3,2,1,0:T(8,128)(2,1)S(1)} copy-done((bf16[16,9,32,128]{3,2,1,0:T(8,128)(2,1)S(1)}, bf16[16,9,32,128]{3,2,1,0:T(8,128)(2,1)}, u32[]{:S(2)}) %copy-start.1) | copy-done | bytes 1179672
  3.4 0.0 copy-start.2
  3.4 0.9 %copy-done.2 = bf16[64,2048]{1,0:T(8,128)(2,1)S(1)} copy-done((bf16[64,2048]{1,0:T(8,128)(2,1)S(1)}, bf16[64,2048]{1,0:T(8,128)(2,1)}, u32[]{:S(2)}) %copy-start.2) | copy-done | bytes 262168
  4.4 0.0 copy-start.3
  4.4 0.9 %copy-done.3 = bf16[64,2048]{1,0:T(8,128)(2,1)S(1)} copy-done((bf16[64,2048]{1,0:T(8,128)(2,1)S(1)}, bf16[64,2048]{1,0:T(8,128)(2,1)}, u32[]{:S(2)}) %copy-start.3) | copy-done | bytes 262168
  5.3 0.0 copy-start.4
  5.3 0.9 %copy-done.4 = bf16[32,2048]{1,0:T(8,128)(2,1)S(1)} copy-done((bf16[32,2048]{1,0:T(8,128)(2,1)S(1)}, bf16[32,2048]{1,0:T(8,128)(2,1)}, u32[]{:S(2)}) %copy-start.4) | copy-done | bytes 131096
  6.2 23.0 %shard_map.64 = f32[32,2048]{1,0:T(8,128)S(1)} custom-call(s32[24,2]{1,0:T(8,128)S(1)} %copy.7.list_ref, bf16[32,2048]{1,0:T(8,128)(2,1)S(1)} %copy-done.4, bf16[64,2048]{1,0:T(8,128)(2,1)S(1)} %copy-done.2, bf16[16,9,32,128]{3,2,1,0:T(8,128)(2,1)S(1)} %copy-done.1, bf16[64,2048]{1,0:T(8,128)(2,1)S(1)} %copy-done.3, bf16[24,128,256]{2,1,0:T(8,128)(2,1)S(1)} %copy-done), custom_call_target="tpu_custom_call" | custom-call | tf_op jit(solution)/shard_map/pallas_call | solution.py:326
  29.2 0.7 %copy.9 = f32[32,2048]{1,0:T(8,128)} copy(f32[32,2048]{1,0:T(8,128)S(1)} %shard_map.64) | data formatting | bytes 524288
Async XLA Ops:
  0.8 1.4 %copy-start = (bf16[24,128,256]{2,1,0:T(8,128)(2,1)S(1)}, bf16[24,128,256]{2,1,0:T(8,128)(2,1)}, u32[]{:S(2)}) copy-start(bf16[24,128,256]{2,1,0:T(8,128)(2,1)} %block_hbm.1) | copy-start | bytes 4718596
  2.2 1.3 %copy-start.1 = (bf16[16,9,32,128]{3,2,1,0:T(8,128)(2,1)S(1)}, bf16[16,9,32,128]{3,2,1,0:T(8,128)(2,1)}, u32[]{:S(2)}) copy-start(bf16[16,9,32,128]{3,2,1,0:T(8,128)(2,1)} %transfer_hbm.1) | copy-start | bytes 3538948
  3.4 0.9 %copy-start.2 = (bf16[64,2048]{1,0:T(8,128)(2,1)S(1)}, bf16[64,2048]{1,0:T(8,128)(2,1)}, u32[]{:S(2)}) copy-start(bf16[64,2048]{1,0:T(8,128)(2,1)} %row_hbm.1) | copy-start | bytes 786436
  4.4 0.9 %copy-start.3 = (bf16[64,2048]{1,0:T(8,128)(2,1)S(1)}, bf16[64,2048]{1,0:T(8,128)(2,1)}, u32[]{:S(2)}) copy-start(bf16[64,2048]{1,0:T(8,128)(2,1)} %column_hbm.1) | copy-start | bytes 786436
  5.3 0.9 %copy-start.4 = (bf16[32,2048]{1,0:T(8,128)(2,1)S(1)}, bf16[32,2048]{1,0:T(8,128)(2,1)}, u32[]{:S(2)}) copy-start(bf16[32,2048]{1,0:T(8,128)(2,1)} %signal_hbm.1) | copy-start | bytes 393220

commit v2 on v1

--- a/solution.py
+++ b/solution.py
@@ -196,7 +196,7 @@
             copy.wait_recv()
         block_copy.wait()
         for s in range(slots):
-            picked = win[jnp.maximum(list_ref[s, 0], 0)]
+            picked = win[jnp.maximum(list_ref[0, s], 0)]
             both = dot(picked, blocks[s])
             vals[s, :rhs] = both[:rhs, :LEAF] + both[rhs:, LEAF:]
             vals[s, rhs:] = both[rhs:, :LEAF] - both[:rhs, LEAF:]
@@ -204,7 +204,7 @@
     def near_sum(j):
         total = jnp.zeros((channels, LEAF), F32)
         for s in range(slots):
-            total = total + jnp.where(list_ref[s, 1] == j, vals[s], 0.0)
+            total = total + jnp.where(list_ref[1, s] == j, vals[s], 0.0)
         near[j] = total
 
     def near_sums(first, stop):
@@ -322,7 +322,7 @@
         rhs = channels // 2
         levels, rank = transfer.shape[1], transfer.shape[2]
         slots = near_blocks.shape[0]
-        anywhere = pl.BlockSpec(memory_space=pl.ANY)
+        anywhere = pl.BlockSpec(memory_space=pltpu.HBM)
         return pl.pallas_call(
             functools.partial(kernel, leaf_count, sub_count),
             out_shape=jax.ShapeDtypeStruct((channels, points), F32),
@@ -349,9 +349,9 @@
                 pltpu.SemaphoreType.DMA((4,)),
             ],
             compiler_params=pltpu.CompilerParams(
-                collective_id=0, has_side_effects=True, vmem_limit_bytes=40 * 1024 * 1024
+                collective_id=0, has_side_effects=True, vmem_limit_bytes=63000000
             ),
-        )(near_list, signal, row_basis, transfer, column_basis, near_blocks)
+        )(near_list.T, signal, row_basis, transfer, column_basis, near_blocks)
 
     return jax.shard_map(
         shards,

time: 30.2 us -> 26 us (0.86)
  local copies, waits for them, and re-layouts: 6.94 us -> 1.67 us
  Pallas kernels: 23 us -> 24.2 us
    unnamed x12 -> x1, local copies, waits for them, and re-layouts: 6.94 us -> 1.67 us
    pallas_call x1, Pallas kernels: 23 us -> 24.2 us  [shards(): pl.pallas_call(functools.partial(kernel, leaf_count, sub_count), out_shap...]
where the time goes in v2:
time: 26 us; the launch traced here: 25.9 us
  Pallas kernels  24.2 us (93%)
  local copies, waits for them, and re-layouts  1.67 us (6%)
    pallas_call x1, Pallas kernels, shards(): pl.pallas_call(functools.partial(kernel, leaf_count, sub_count), out_shap...  24.2 us
    unnamed x1, local copies, waits for them, and re-layouts  1.67 us

profile of v2, /device:TPU:0, one launch (start us, length us, event | category | flops | bytes accessed | tf_op | source)
XLA Modules:
  0.0 25.9 jit_solution(9056381553896008304)
XLA Ops:
  0.0 24.2 %shard_map.64 = f32[32,2048]{1,0:T(8,128)} custom-call(s32[2,24]{1,0:T(2,128)} %bitcast.1, bf16[32,2048]{1,0:T(8,128)(2,1)} %signal_hbm.1, bf16[64,2048]{1,0:T(8,128)(2,1)} %row_hbm.1, bf16[16,9,32,128]{3,2,1,0:T(8,128)(2,1)} %transfer_hbm.1, bf16[64,2048]{1,0:T(8,128)(2,1)} %column_hbm.1, bf16[24,128,256]{2,1,0:T(8,128)(2,1)} %block_hbm.1), custom_call_target="tpu_custom_call" | custom-call | tf_op jit(solution)/shard_map/pallas_call | solution.py:326
  24.2 1.7 %copy.8 = f32[32,2048]{1,0:T(8,128)} copy(f32[32,2048]{1,0:T(8,128)} %shard_map.64) | data formatting | bytes 524288

commit v3 on v2

--- a/solution.py
+++ b/solution.py
@@ -81,11 +81,11 @@
         pltpu.make_async_copy(transfer_hbm.at[:, l], transfer.at[l], in_sems.at[boxes + 3 + l])
         for l in range(levels)
     ]
+    for l in range(local_levels):
+        transfer_copies[l].start()
     for copy in signal_copies:
         copy.start()
     row_copy.start()
-    for l in range(local_levels):
-        transfer_copies[l].start()
 
     barrier = pltpu.get_barrier_semaphore()
     for partner in partners:
@@ -133,25 +133,11 @@
 
     left = lax.broadcasted_iota(jnp.int32, (rhs, LEAF), 1) < wide
 
+    for l in range(local_levels):
+        build(l)
+
     for copy in signal_copies:
         copy.wait()
-    pl.semaphore_wait(barrier, len(partners))
-    halo = [
-        pltpu.make_async_remote_copy(
-            src_ref=win.at[pl.ds(boxes, 2 * reach)], dst_ref=win.at[pl.ds(0, 2 * reach)],
-            send_sem=halo_send.at[0], recv_sem=halo_recv.at[0],
-            device_id=next_id, device_id_type=MESH,
-        ),
-        pltpu.make_async_remote_copy(
-            src_ref=win.at[pl.ds(2 * reach, 2 * reach)],
-            dst_ref=win.at[pl.ds(2 * reach + boxes, 2 * reach)],
-            send_sem=halo_send.at[1], recv_sem=halo_recv.at[1],
-            device_id=prev_id, device_id_type=MESH,
-        ),
-    ]
-    for copy in halo:
-        copy.start()
-
     row_copy.wait()
     coeffs = []
     for k in range(pairs):
@@ -170,8 +156,23 @@
         )
         coeffs.append(jnp.where(left, both[:rhs], both[rhs:]))
 
-    for l in range(local_levels):
-        build(l)
+    pl.semaphore_wait(barrier, len(partners))
+    halo = [
+        pltpu.make_async_remote_copy(
+            src_ref=win.at[pl.ds(boxes, 2 * reach)], dst_ref=win.at[pl.ds(0, 2 * reach)],
+            send_sem=halo_send.at[0], recv_sem=halo_recv.at[0],
+            device_id=next_id, device_id_type=MESH,
+        ),
+        pltpu.make_async_remote_copy(
+            src_ref=win.at[pl.ds(2 * reach, 2 * reach)],
+            dst_ref=win.at[pl.ds(2 * reach + boxes, 2 * reach)],
+            send_sem=halo_send.at[1], recv_sem=halo_recv.at[1],
+            device_id=prev_id, device_id_type=MESH,
+        ),
+    ]
+    for copy in halo:
+        copy.start()
+
     for l in range(local_levels - 1):
         bit = 1 << l
         coeffs = [
@@ -251,8 +252,8 @@
 
     steps = len(crossing)
     extra = [[] for _ in range(steps)]
-    extra[min(1, steps - 1)].append(near_edges)
-    extra[min(2, steps - 1)].append(near_middle)
+    extra[min(2, steps - 1)].append(near_edges)
+    extra[min(3, steps - 1)].append(near_middle)
     extra[min(3, steps - 1)].append(build_evals)
 
     for part in range(CHUNKS):

time: 26 us -> 26.1 us (level)
  no operation moved by 1% of the time
where the time goes in v3:
time: 26.1 us; the launch traced here: 25.9 us
  Pallas kernels  24.2 us (93%)
  local copies, waits for them, and re-layouts  1.67 us (6%)
    pallas_call x1, Pallas kernels, shards(): pl.pallas_call(functools.partial(kernel, leaf_count, sub_count), out_shap...  24.2 us
    unnamed x1, local copies, waits for them, and re-layouts  1.67 us

profile of v3, /device:TPU:0, one launch (start us, length us, event | category | flops | bytes accessed | tf_op | source)
XLA Modules:
  0.0 25.9 jit_solution(16678595775931697181)
XLA Ops:
  0.0 24.2 %shard_map.64 = f32[32,2048]{1,0:T(8,128)} custom-call(s32[2,24]{1,0:T(2,128)} %bitcast.1, bf16[32,2048]{1,0:T(8,128)(2,1)} %signal_hbm.1, bf16[64,2048]{1,0:T(8,128)(2,1)} %row_hbm.1, bf16[16,9,32,128]{3,2,1,0:T(8,128)(2,1)} %transfer_hbm.1, bf16[64,2048]{1,0:T(8,128)(2,1)} %column_hbm.1, bf16[24,128,256]{2,1,0:T(8,128)(2,1)} %block_hbm.1), custom_call_target="tpu_custom_call" | custom-call | tf_op jit(solution)/shard_map/pallas_call | solution.py:327
  24.2 1.7 %copy.8 = f32[32,2048]{1,0:T(8,128)} copy(f32[32,2048]{1,0:T(8,128)} %shard_map.64) | data formatting | bytes 524288
